TPU v7x, 32 devices: a whole 2x2x4 slice. The times are simulated.
32 devices in a mesh: dp: 8 (over z, y), tensor: 4 (over x, core).
Axes of the slice: x: 2, y: 2, z: 4, core: 2. Of those that a mesh axis runs over, the one named last changes fastest.
Arguments:
- tokens: bfloat16 [8192, 2048], P(('dp', 'tensor')), may hold values from -6 to 6
- lengths: int32 [8], P('dp'), may hold values from 256 to 1024, as said below
- attn_gain: bfloat16 [2048], replicated, may hold values from 0.25 to 1.75
- w_query: bfloat16 [2048, 2048], P('dp', 'tensor'), may hold values from -0.125 to 0.125
- w_key: bfloat16 [2048, 512], P('dp', 'tensor'), may hold values from -0.125 to 0.125
- w_value: bfloat16 [2048, 512], P('dp', 'tensor'), may hold values from -0.125 to 0.125
- w_output: bfloat16 [2048, 2048], P('tensor', 'dp'), may hold values from -1 to 1
- mlp_gain: bfloat16 [2048], replicated, may hold values from 0.25 to 1.75
- w_gate: bfloat16 [2048, 8192], P('dp', 'tensor'), may hold values from -0.125 to 0.125
- w_up: bfloat16 [2048, 8192], P('dp', 'tensor'), may hold values from -0.125 to 0.125
- w_down: bfloat16 [8192, 2048], P('tensor', 'dp'), may hold values from -0.125 to 0.125
- cotangent: bfloat16 [8192, 2048], P(('dp', 'tensor')), may hold values from -6 to 6
Outputs:
- layer_out: bfloat16 [8192, 2048], P(('dp', 'tensor'))
- grad_tokens: float32 [8192, 2048], P(('dp', 'tensor'))
- grad_query: float32 [2048, 2048], P('dp', 'tensor')
- grad_key: float32 [2048, 512], P('dp', 'tensor')
- grad_value: float32 [2048, 512], P('dp', 'tensor')
- grad_output: float32 [2048, 2048], P('tensor', 'dp')
- grad_gate: float32 [2048, 8192], P('dp', 'tensor')
- grad_up: float32 [2048, 8192], P('dp', 'tensor')
- grad_down: float32 [8192, 2048], P('tensor', 'dp')
- grad_attn_gain: float32 [2048], P(('dp', 'tensor'))
- grad_mlp_gain: float32 [2048], P(('dp', 'tensor'))
Inputs may be any that keep to these rules, and one draw needn't show every extreme that they name: `lengths`: each of the 8 sequences has a valid length from 256 to 1024; at least one has length exactly 1024.
All inputs are finite; a program needn't handle non-finite values.
Results may differ from a plain program's by a relative error of at most 0.015.
Values may be sent and summed in bfloat16 or wider, within the bound.
A program may use at most 192 MiB of HBM per device.

v0:
```python
import jax
import jax.numpy as jnp
from jax import lax
from jax.sharding import PartitionSpec as P

HD = 64
LEN = 1024
epsilon = 1e-05
theta = 500000.0


def rope_frequencies():
    half_size = HD // 2
    base_freq = theta ** (-(jnp.arange(half_size, dtype=jnp.float32) * 2.0) / HD)
    wavelength = 2.0 * jnp.pi / base_freq
    smooth = (8192.0 / wavelength - 1.0) / 3.0
    middle = (1.0 - smooth) * base_freq / 32.0 + smooth * base_freq
    return jnp.where(
        wavelength < 2048.0, base_freq, jnp.where(wavelength > 8192.0, base_freq / 32.0, middle)
    )


def rope_tables(positions):
    frequency = rope_frequencies()
    angles = positions.astype(jnp.float32)[:, None] * frequency[None, :]
    angles = jnp.concatenate([angles, angles], axis=1)
    return (jnp.cos(angles), jnp.sin(angles))


def rotate_half(vector):
    half_size = vector.shape[-1] // 2
    return jnp.concatenate([-vector[..., half_size:], vector[..., :half_size]], axis=-1)


def rope_apply(vector, cosine_table, sine_table):
    return vector * cosine_table[:, None, :] + rotate_half(vector) * sine_table[:, None, :]


def rope_back(grads, cosine_table, sine_table):
    return grads * cosine_table[:, None, :] - rotate_half(grads * sine_table[:, None, :])


def gather_attention(w_query, w_key, w_value, w_output):
    return (
        lax.all_gather(w_query, "dp", axis=0, tiled=True),
        lax.all_gather(w_key, "dp", axis=0, tiled=True),
        lax.all_gather(w_value, "dp", axis=0, tiled=True),
        lax.all_gather(w_output, "dp", axis=1, tiled=True),
    )


def gather_mlp(w_gate, w_up, w_down):
    return (
        lax.all_gather(w_gate, "dp", axis=0, tiled=True),
        lax.all_gather(w_up, "dp", axis=0, tiled=True),
        lax.all_gather(w_down, "dp", axis=1, tiled=True),
    )


def add_rows(accum, piece):
    return accum + piece


def block_scores(queries, key_vecs, lengths, block_index, block_rows):
    per_seq = LEN // block_rows
    sequence = block_index // per_seq
    row_start = block_index * block_rows
    query_blk = lax.dynamic_slice_in_dim(queries, row_start, block_rows, 0)
    length = lax.dynamic_index_in_dim(lengths, sequence, 0, keepdims=False)
    scores = jnp.einsum(
        "qkrd,jkd->krqj", query_blk, key_vecs, preferred_element_type=jnp.float32
    ) * HD ** (-0.5)
    query_pos = row_start % LEN + jnp.arange(block_rows)
    key_pos = jnp.arange(LEN)
    allowed = (key_pos[None, :] <= query_pos[:, None]) & (key_pos[None, :] < length)
    return (jnp.where(allowed, scores, -1e30), sequence, row_start, query_blk, key_vecs)


def attend(queries, key_vecs, values, lengths):
    total_rows = queries.shape[0]
    block_rows = min(512, LEN)
    blocks = total_rows // block_rows

    def one_block(block_index):
        scores, sequence, row_start, query_blk, key_seq = block_scores(
            queries, key_vecs, lengths, block_index, block_rows
        )
        row_max = jnp.max(scores, axis=-1, keepdims=True)
        exp_scores = jnp.exp(scores - row_max)
        denom = jnp.sum(exp_scores, axis=-1, keepdims=True)
        soft_low = (exp_scores / denom).astype(jnp.bfloat16)
        result = jnp.einsum("krqj,jkd->qkrd", soft_low, values, preferred_element_type=jnp.float32)
        return (result, row_max[..., 0] + jnp.log(denom[..., 0]))

    results, logsum = lax.map(one_block, jnp.arange(blocks, dtype=jnp.int32))
    return (results.reshape((total_rows,) + queries.shape[1:]), logsum)


def attend_back(queries, key_vecs, values, grad_heads, logsum, lengths):
    total_rows = queries.shape[0]
    block_rows = min(512, LEN)
    blocks = total_rows // block_rows

    def one_block(carry, item):
        key_acc, value_acc = carry
        block_index, logsum_blk = item
        scores, sequence, row_start, query_blk, key_seq = block_scores(
            queries, key_vecs, lengths, block_index, block_rows
        )
        grad_blk = lax.dynamic_slice_in_dim(grad_heads, row_start, block_rows, 0)
        soft_weights = jnp.exp(scores - logsum_blk[..., None])
        grad_soft = jnp.einsum(
            "qkrd,jkd->krqj", grad_blk, values, preferred_element_type=jnp.float32
        )
        inner_sum = jnp.sum(soft_weights * grad_soft, axis=-1, keepdims=True)
        grad_scores = (soft_weights * (grad_soft - inner_sum)).astype(jnp.bfloat16)
        grad_query = jnp.einsum(
            "krqj,jkd->qkrd", grad_scores, key_seq, preferred_element_type=jnp.float32
        ) * HD ** (-0.5)
        grad_keyblk = jnp.einsum(
            "krqj,qkrd->jkd", grad_scores, query_blk, preferred_element_type=jnp.float32
        ) * HD ** (-0.5)
        grad_valblk = jnp.einsum(
            "krqj,qkrd->jkd",
            soft_weights.astype(jnp.bfloat16),
            grad_blk,
            preferred_element_type=jnp.float32,
        )
        key_acc = add_rows(key_acc, grad_keyblk)
        value_acc = add_rows(value_acc, grad_valblk)
        return ((key_acc, value_acc), grad_query)

    zero_keys = jnp.zeros(key_vecs.shape, jnp.float32)
    (grad_keys, grad_values), grad_queries = lax.scan(
        one_block, (zero_keys, zero_keys), (jnp.arange(blocks, dtype=jnp.int32), logsum)
    )
    return (grad_queries.reshape((total_rows,) + queries.shape[1:]), grad_keys, grad_values)


def body(
    tokens,
    lengths,
    attn_gain,
    w_query,
    w_key,
    w_value,
    w_output,
    mlp_gain,
    w_gate,
    w_up,
    w_down,
    cotangent,
):
    local_rows = tokens.shape[0]
    token_full = tokens.astype(jnp.float32)
    gain_attn = attn_gain.astype(jnp.float32)
    gain_mlp = mlp_gain.astype(jnp.float32)
    inv_first = lax.rsqrt(jnp.mean(token_full * token_full, axis=1, keepdims=True) + epsilon)
    normed_attn = (token_full * inv_first * gain_attn).astype(jnp.bfloat16)
    rows_attn = lax.all_gather(normed_attn, "tensor", axis=0, tiled=True)
    group_rows = rows_attn.shape[0]
    cosine_table, sine_table = rope_tables(jnp.arange(group_rows) % LEN)
    query_all, key_all, value_all, output_all = gather_attention(w_query, w_key, w_value, w_output)
    heads_local = query_all.shape[1] // HD
    kv_local = key_all.shape[1] // HD
    query_pre = jnp.dot(rows_attn, query_all, preferred_element_type=jnp.float32)
    key_pre = jnp.dot(rows_attn, key_all, preferred_element_type=jnp.float32)
    values = (
        jnp.dot(rows_attn, value_all, preferred_element_type=jnp.float32)
        .astype(jnp.bfloat16)
        .reshape(group_rows, kv_local, HD)
    )
    queries = rope_apply(
        query_pre.reshape(group_rows, heads_local, HD), cosine_table, sine_table
    ).astype(jnp.bfloat16)
    queries = queries.reshape(group_rows, kv_local, heads_local // kv_local, HD)
    key_vecs = rope_apply(
        key_pre.reshape(group_rows, kv_local, HD), cosine_table, sine_table
    ).astype(jnp.bfloat16)
    head_full, logsum = attend(queries, key_vecs, values, lengths)
    head_out = head_full.reshape(group_rows, heads_local * HD).astype(jnp.bfloat16)
    picked = head_out
    attn_branch = lax.psum_scatter(
        jnp.dot(picked, output_all, preferred_element_type=jnp.float32),
        "tensor",
        scatter_dimension=0,
        tiled=True,
    )
    hidden = token_full + attn_branch
    inv_second = lax.rsqrt(jnp.mean(hidden * hidden, axis=1, keepdims=True) + epsilon)
    normed_mlp = (hidden * inv_second * gain_mlp).astype(jnp.bfloat16)
    rows_mlp = lax.all_gather(normed_mlp, "tensor", axis=0, tiled=True)
    gate_all, up_all, down_all = gather_mlp(w_gate, w_up, w_down)
    gate_proj = jnp.dot(rows_mlp, gate_all, preferred_element_type=jnp.float32)
    up_proj = jnp.dot(rows_mlp, up_all, preferred_element_type=jnp.float32)
    gate_sig = jax.nn.sigmoid(gate_proj)
    activated = (gate_proj * gate_sig * up_proj).astype(jnp.bfloat16)
    picked = activated
    mlp_branch = lax.psum_scatter(
        jnp.dot(picked, down_all, preferred_element_type=jnp.float32).astype(jnp.bfloat16),
        "tensor",
        scatter_dimension=0,
        tiled=True,
    ).astype(jnp.float32)
    layer_out = (hidden + mlp_branch).astype(jnp.bfloat16)
    group_row = lax.axis_index("tensor") * local_rows + jnp.arange(local_rows)
    row_seq = group_row // LEN
    row_pos = group_row % LEN
    seq_ids = jnp.arange(lengths.shape[0])
    row_len = jnp.sum(jnp.where(row_seq[:, None] == seq_ids[None, :], lengths[None, :], 0), axis=1)
    valid_rows = (row_pos < row_len).astype(jnp.float32)
    cot_masked = cotangent.astype(jnp.float32) * valid_rows[:, None]
    gate_all, up_all, down_all = gather_mlp(w_gate, w_up, w_down)
    grad_branch = lax.all_gather(cot_masked.astype(jnp.bfloat16), "tensor", axis=0, tiled=True)
    grad_down = jnp.einsum("gf,gd->fd", activated, grad_branch, preferred_element_type=jnp.float32)
    grad_act = jnp.einsum("gd,fd->gf", grad_branch, down_all, preferred_element_type=jnp.float32)
    grad_gate_pre = (grad_act * up_proj * gate_sig * (1.0 + gate_proj * (1.0 - gate_sig))).astype(
        jnp.bfloat16
    )
    grad_up_pre = (grad_act * gate_proj * gate_sig).astype(jnp.bfloat16)
    grad_gate = jnp.einsum("gd,gf->df", rows_mlp, grad_gate_pre, preferred_element_type=jnp.float32)
    grad_up = jnp.einsum("gd,gf->df", rows_mlp, grad_up_pre, preferred_element_type=jnp.float32)
    grad_gate, grad_up, grad_down = (
        lax.psum_scatter(grad_gate, "dp", scatter_dimension=0, tiled=True),
        lax.psum_scatter(grad_up, "dp", scatter_dimension=0, tiled=True),
        lax.psum_scatter(grad_down, "dp", scatter_dimension=1, tiled=True),
    )
    grad_norm_two = lax.psum_scatter(
        jnp.einsum("gf,df->gd", grad_gate_pre, gate_all, preferred_element_type=jnp.float32)
        + jnp.einsum("gf,df->gd", grad_up_pre, up_all, preferred_element_type=jnp.float32),
        "tensor",
        scatter_dimension=0,
        tiled=True,
    )
    scaled_two = grad_norm_two * gain_mlp
    gain_two_part = jnp.sum(grad_norm_two * hidden * inv_second, axis=0)
    grad_hidden = (
        cot_masked
        + inv_second * scaled_two
        - hidden * inv_second**3 * jnp.mean(scaled_two * hidden, axis=1, keepdims=True)
    )
    query_all, key_all, value_all, output_all = gather_attention(w_query, w_key, w_value, w_output)
    grad_attn = lax.all_gather(grad_hidden.astype(jnp.bfloat16), "tensor", axis=0, tiled=True)
    grad_output = jnp.einsum("gh,gd->hd", head_out, grad_attn, preferred_element_type=jnp.float32)
    grad_heads = jnp.einsum(
        "gd,hd->gh", grad_attn, output_all, preferred_element_type=jnp.float32
    ).astype(jnp.bfloat16)
    grad_heads = grad_heads.reshape(group_rows, kv_local, heads_local // kv_local, HD)
    grad_queries, grad_keys, grad_values = attend_back(
        queries, key_vecs, values, grad_heads, logsum, lengths
    )
    grad_qpre = rope_back(
        grad_queries.reshape(group_rows, heads_local, HD), cosine_table, sine_table
    )
    grad_qpre = grad_qpre.astype(jnp.bfloat16).reshape(group_rows, heads_local * HD)
    grad_kpre = (
        rope_back(grad_keys, cosine_table, sine_table)
        .astype(jnp.bfloat16)
        .reshape(group_rows, kv_local * HD)
    )
    grad_vpre = grad_values.astype(jnp.bfloat16).reshape(group_rows, kv_local * HD)
    grad_query = jnp.einsum("gd,gh->dh", rows_attn, grad_qpre, preferred_element_type=jnp.float32)
    grad_key = jnp.einsum("gd,gh->dh", rows_attn, grad_kpre, preferred_element_type=jnp.float32)
    grad_value = jnp.einsum("gd,gh->dh", rows_attn, grad_vpre, preferred_element_type=jnp.float32)
    grad_query, grad_key, grad_value, grad_output = (
        lax.psum_scatter(grad_query, "dp", scatter_dimension=0, tiled=True),
        lax.psum_scatter(grad_key, "dp", scatter_dimension=0, tiled=True),
        lax.psum_scatter(grad_value, "dp", scatter_dimension=0, tiled=True),
        lax.psum_scatter(grad_output, "dp", scatter_dimension=1, tiled=True),
    )
    grad_norm_one = lax.psum_scatter(
        jnp.einsum("gh,dh->gd", grad_qpre, query_all, preferred_element_type=jnp.float32)
        + jnp.einsum("gh,dh->gd", grad_kpre, key_all, preferred_element_type=jnp.float32)
        + jnp.einsum("gh,dh->gd", grad_vpre, value_all, preferred_element_type=jnp.float32),
        "tensor",
        scatter_dimension=0,
        tiled=True,
    )
    scaled_one = grad_norm_one * gain_attn
    gain_one_part = jnp.sum(grad_norm_one * token_full * inv_first, axis=0)
    grad_tokens = (
        grad_hidden
        + inv_first * scaled_one
        - token_full * inv_first**3 * jnp.mean(scaled_one * token_full, axis=1, keepdims=True)
    )
    grad_attn_gain, grad_mlp_gain = (
        lax.psum_scatter(gain_one_part, ("dp", "tensor"), scatter_dimension=0, tiled=True),
        lax.psum_scatter(gain_two_part, ("dp", "tensor"), scatter_dimension=0, tiled=True),
    )
    return (
        layer_out,
        grad_tokens,
        grad_query,
        grad_key,
        grad_value,
        grad_output,
        grad_gate,
        grad_up,
        grad_down,
        grad_attn_gain,
        grad_mlp_gain,
    )


def solution(mesh):
    in_specs = (
        P(("dp", "tensor"), None),
        P("dp"),
        P(),
        P("dp", "tensor"),
        P("dp", "tensor"),
        P("dp", "tensor"),
        P("tensor", "dp"),
        P(),
        P("dp", "tensor"),
        P("dp", "tensor"),
        P("tensor", "dp"),
        P(("dp", "tensor"), None),
    )
    out_specs = (
        P(("dp", "tensor"), None),
        P(("dp", "tensor"), None),
        P("dp", "tensor"),
        P("dp", "tensor"),
        P("dp", "tensor"),
        P("tensor", "dp"),
        P("dp", "tensor"),
        P("dp", "tensor"),
        P("tensor", "dp"),
        P(("dp", "tensor")),
        P(("dp", "tensor")),
    )
    return jax.shard_map(body, mesh=mesh, in_specs=in_specs, out_specs=out_specs, check_vma=False)
```

profile of v0, /device:TPU:0, one launch (start us, length us, event | category | flops | bytes accessed | tf_op | source)
XLA Modules:
  0.0 2289.9 jit_solution(13640120241173803262)
XLA Ops:
  15.9 33.1 %all_gather.42 = bf16[2048,128]{1,0:T(8,128)(2,1)S(1)} all-gather(bf16[256,128]{1,0:T(8,128)(2,1)S(1)} %copy-done.27), channel_id=1, replica_groups=mesh['dp'=8,'tensor'=4] {'dp'}, dimensions={0}, use_global_device_ids=true | all-gather | bytes 589824 | tf_op jit(solution)/shard_map/all_gather | solution.py:46
  49.0 31.9 %all_gather.43 = bf16[2048,128]{1,0:T(8,128)(2,1)S(1)} all-gather(bf16[256,128]{1,0:T(8,128)(2,1)S(1)} %copy-done.28), channel_id=1, replica_groups=mesh['dp'=8,'tensor'=4] {'dp'}, dimensions={0}, use_global_device_ids=true | all-gather | bytes 589824 | tf_op jit(solution)/shard_map/all_gather | solution.py:47
  113.4 33.0 %while.31 = (s32[]{:T(128)}, bf16[2,512,2,4,64]{1,4,3,2,0:T(8,128)(2,1)S(1)}, f32[2,2,4,512]{3,2,1,0:T(4,128)}, s32[2]{0:T(128)S(1)}, s32[1]{0:T(128)}, /*index=...) while((s32[]{:T(128)}, ...), condition=%wide.region_4.5_spmd, body=%wide.region_1.4_spmd.sunk | while | flops 1125119488 | bytes 54663480 | solution.py:95
  162.1 69.1 %reduce-scatter.12.cloned.1.call-done = f32[256,2048]{1,0:T(8,128)} async-done(((f32[1024,2048]{1,0:T(8,128)}), f32[256,2048]{1,0:T(8,128)}) %reduce-scatter.12.cloned.1.call-update) | async-done | bytes 2097168 | tf_op jit(solution)/shard_map/reduce_scatter | solution.py:183
  239.1 118.6 %all-gather.20.cloned.1.call-done = bf16[2048,2048]{1,0:T(8,128)(2,1)} async-done(((bf16[256,2048]{1,0:T(8,128)(2,1)}), bf16[2048,2048]{1,0:T(8,128)(2,1)}) %all-gather.20.cloned.1.call-update) | async-done | bytes 8388624 | tf_op jit(solution)/shard_map/all_gather | solution.py:55
  357.7 34.7 %all-gather.16.cloned.1.call-done = bf16[1024,2048]{1,0:T(8,128)(2,1)} async-done(((bf16[256,2048]{1,0:T(8,128)(2,1)}), bf16[1024,2048]{1,0:T(8,128)(2,1)}) %all-gather.16.cloned.1.call-update) | async-done | bytes 4194320 | tf_op jit(solution)/shard_map/all_gather | solution.py:192
  407.3 111.7 %all-gather.18.cloned.1.call-done = bf16[2048,2048]{1,0:T(8,128)(2,1)} async-done(((bf16[256,2048]{1,0:T(8,128)(2,1)}), bf16[2048,2048]{1,0:T(8,128)(2,1)}) %all-gather.18.cloned.1.call-update) | async-done | bytes 8388624 | tf_op jit(solution)/shard_map/all_gather | solution.py:54
  533.5 20.3 all-gather.24.cloned.1.call-done
  553.8 127.0 %all-gather.22.cloned.1.call-done = bf16[2048,2048]{1,0:T(8,128)(2,1)} async-done(((bf16[2048,256]{1,0:T(8,128)(2,1)}), bf16[2048,2048]{1,0:T(8,128)(2,1)}) %all-gather.22.cloned.1.call-update) | async-done | bytes 8388624 | tf_op jit(solution)/shard_map/all_gather | solution.py:56
  680.8 22.1 multiply_convert_fusion
  743.5 55.7 %reduce-scatter.16.cloned.1.call-done = f32[256,2048]{1,0:T(8,128)} async-done(((f32[1024,2048]{1,0:T(8,128)}), f32[256,2048]{1,0:T(8,128)}) %reduce-scatter.16.cloned.1.call-update) | async-done | bytes 2097168 | tf_op jit(solution)/shard_map/reduce_scatter | solution.py:228
  801.9 44.4 %reduce-scatter.14.cloned.1.call-done = bf16[256,2048]{1,0:T(8,128)(2,1)} async-done(((bf16[1024,2048]{1,0:T(8,128)(2,1)}), bf16[256,2048]{1,0:T(8,128)(2,1)}) %reduce-scatter.14.cloned.1.call-update) | async-done | bytes 1048592 | tf_op jit(solution)/shard_map/reduce_scatter | solution.py:199
  851.1 34.5 %all-gather.26.cloned.1.call-done = bf16[1024,2048]{1,0:T(8,128)(2,1)} async-done(((bf16[256,2048]{1,0:T(8,128)(2,1)}), bf16[1024,2048]{1,0:T(8,128)(2,1)}) %all-gather.26.cloned.1.call-update) | async-done | bytes 4194320 | tf_op jit(solution)/shard_map/all_gather | solution.py:243
  891.8 129.4 %while.32 = (s32[]{:T(128)}, f32[1024,2,64]{0,2,1:T(8,128)S(1)}, f32[1024,2,64]{0,2,1:T(8,128)}, f32[2,512,2,4,64]{1,0,4,3,2:T(2,128)}, s32[2]{0:T(128)S(1)}, /*...) while((s32[]{:T(128)}, f32[1024,2,64]{0,2,1:T(8,128)S(1)}, ...), condition=%wide.region_12.13_spmd.clone, body=%wide.region_10.12_spmd.clone.sunk | while | flops 2749232640 | bytes 176085424 | solution.py:134
  936.5 19.6 dynamic_update_slice.28
  1001.5 19.6 dynamic_update_slice.28
  1115.1 39.9 %all-reduce.2 = (f32[2048]{0:T(1024)S(1)}, f32[2048]{0:T(1024)S(1)}) all-reduce(f32[2048]{0:T(1024)S(1)} %get-tuple-element.297, f32[2048]{0:T(1024)S(1)} %copy-done.29), channel_id=13, replica_groups=mesh['dp'=8,'tensor'=4] {'dp','tensor'}, use_global_device_ids=true, to_apply=%region_23.24.clone | all-reduce | flops 4096 | bytes 32768
  1159.7 20.7 reduce-scatter.22.cloned.1.call-done
  1180.4 67.1 %reduce-scatter.24.cloned.1.call-done = f32[256,128]{1,0:T(8,128)} async-done(((f32[2048,128]{1,0:T(8,128)}), f32[256,128]{1,0:T(8,128)}) %reduce-scatter.24.cloned.1.call-update) | async-done | bytes 131088 | tf_op jit(solution)/shard_map/reduce_scatter | solution.py:268
  1247.5 91.8 %reduce-scatter.26.cloned.1.call-done = f32[512,256]{1,0:T(8,128)} async-done(((f32[512,2048]{1,0:T(8,128)}), f32[512,256]{1,0:T(8,128)}) %reduce-scatter.26.cloned.1.call-update) | async-done | bytes 524304 | tf_op jit(solution)/shard_map/reduce_scatter | solution.py:269
  1339.2 92.0 %reduce-scatter.20.cloned.1.call-done = f32[256,512]{1,0:T(8,128)} async-done(((f32[2048,512]{1,0:T(8,128)}), f32[256,512]{1,0:T(8,128)}) %reduce-scatter.20.cloned.1.call-update) | async-done | bytes 524304 | tf_op jit(solution)/shard_map/reduce_scatter | solution.py:266
  1431.3 284.1 %reduce-scatter.30.cloned.1.call-done = f32[256,2048]{1,0:T(8,128)} async-done(((f32[2048,2048]{1,0:T(8,128)}), f32[256,2048]{1,0:T(8,128)}) %reduce-scatter.30.cloned.1.call-update) | async-done | bytes 2097168 | tf_op jit(solution)/shard_map/reduce_scatter | solution.py:225
  1715.4 283.7 %reduce-scatter.28.cloned.1.call-done = f32[256,2048]{1,0:T(8,128)} async-done(((f32[2048,2048]{1,0:T(8,128)}), f32[256,2048]{1,0:T(8,128)}) %reduce-scatter.28.cloned.1.call-update) | async-done | bytes 2097168 | tf_op jit(solution)/shard_map/reduce_scatter | solution.py:224
  1999.1 283.5 %reduce-scatter.32.cloned.1.call-done = f32[2048,256]{1,0:T(8,128)} async-done(((f32[2048,2048]{1,0:T(8,128)}), f32[2048,256]{1,0:T(8,128)}) %reduce-scatter.32.cloned.1.call-update) | async-done | bytes 2097168 | tf_op jit(solution)/shard_map/reduce_scatter | solution.py:226
  (227 shorter events, 365.3 us)
Async XLA Ops:
  7.2 73.7 %all-gather.10.cloned.1.call-start = ((), (), s32[]{:S(2)}) async-start(), calls=%async_computation.11 | async-start | bytes 5242880 | tf_op jit(solution)/shard_map/all_gather | solution.py:160
  13.2 90.1 %all-gather.12.cloned.1.call-start = ((), (), s32[]{:S(2)}) async-start(), calls=%async_computation.12 | async-start | bytes 2359296 | tf_op jit(solution)/shard_map/all_gather | solution.py:45
  13.9 140.3 %all-gather.14.cloned.1.call-start = ((), (), s32[]{:S(2)}) async-start(), calls=%async_computation.13 | async-start | bytes 2359296 | tf_op jit(solution)/shard_map/all_gather | solution.py:48
  14.7 216.5 %reduce-scatter.12.cloned.1.call-start = ((), (), s32[]{:S(2)}) async-start(), calls=%async_computation.14 | async-start | bytes 10485760 | tf_op jit(solution)/shard_map/reduce_scatter | solution.py:183
  15.8 94.5 %copy-start.9 = (f32[1024,64]{0,1:T(8,128)}, f32[1024,64]{0,1:T(8,128)S(1)}, u32[]{:S(2)}) copy-start(f32[1024,64]{0,1:T(8,128)S(1)} %get-tuple-element.360) | copy-start | bytes 786436
  15.8 94.5 %copy-start.11 = (f32[1024,64]{0,1:T(8,128)}, f32[1024,64]{0,1:T(8,128)S(1)}, u32[]{:S(2)}) copy-start(f32[1024,64]{0,1:T(8,128)S(1)} %get-tuple-element.359) | copy-start | bytes 786436
  161.4 69.8 %copy-start.2 = (bf16[256,2048]{1,0:T(8,128)(2,1)S(1)}, bf16[256,2048]{1,0:T(8,128)(2,1)}, u32[]{:S(2)}) copy-start(bf16[256,2048]{1,0:T(8,128)(2,1)} %param.16) | copy-start | bytes 3145732
  161.5 196.2 %all-gather.20.cloned.1.call-start = ((), (), s32[]{:S(2)}) async-start(), calls=%async_computation.17 | async-start | bytes 9437184 | tf_op jit(solution)/shard_map/all_gather | solution.py:55
  162.1 230.3 %all-gather.16.cloned.1.call-start = ((), (), s32[]{:S(2)}) async-start(), calls=%async_computation.15 | async-start | bytes 5242880 | tf_op jit(solution)/shard_map/all_gather | solution.py:192
  234.4 284.6 %all-gather.18.cloned.1.call-start = ((), (), s32[]{:S(2)}) async-start(), calls=%async_computation.16 | async-start | bytes 9437184 | tf_op jit(solution)/shard_map/all_gather | solution.py:54
  235.2 318.6 %all-gather.24.cloned.1.call-start = ((), (), s32[]{:S(2)}) async-start(), calls=%async_computation.20 | async-start | bytes 5242880 | tf_op jit(solution)/shard_map/all_gather | solution.py:214
  238.3 442.5 %all-gather.22.cloned.1.call-start = ((), (), s32[]{:S(2)}) async-start(), calls=%async_computation.18 | async-start | bytes 9437184 | tf_op jit(solution)/shard_map/all_gather | solution.py:56
  239.1 560.1 %reduce-scatter.16.cloned.1.call-start = ((), (), s32[]{:S(2)}) async-start(), calls=%async_computation.21 | async-start | bytes 10485760 | tf_op jit(solution)/shard_map/reduce_scatter | solution.py:228
  729.4 116.9 %reduce-scatter.14.cloned.1.call-start = ((), (), s32[]{:S(2)}) async-start(), calls=%async_computation.19 | async-start | bytes 5242880 | tf_op jit(solution)/shard_map/reduce_scatter | solution.py:199
  743.4 102.9 %copy-start.17 = (bf16[256,2048]{1,0:T(8,128)(2,1)S(1)}, bf16[256,2048]{1,0:T(8,128)(2,1)}, u32[]{:S(2)}) copy-start(bf16[256,2048]{1,0:T(8,128)(2,1)} %param.27) | copy-start | bytes 3145732
  743.4 142.2 %all-gather.26.cloned.1.call-start = ((), (), s32[]{:S(2)}) async-start(), calls=%async_computation.22 | async-start | bytes 5242880 | tf_op jit(solution)/shard_map/all_gather | solution.py:243
  851.0 261.2 %reduce-scatter.18.cloned.1.call-start = ((), (), s32[]{:S(2)}) async-start(), calls=%async_computation.23 | async-start | bytes 10485760 | tf_op jit(solution)/shard_map/reduce_scatter | solution.py:271
  1040.6 139.8 %reduce-scatter.22.cloned.1.call-start = ((), (), s32[]{:S(2)}) async-start(), calls=%async_computation.25 | async-start | bytes 1179648 | tf_op jit(solution)/shard_map/reduce_scatter | solution.py:267
  1045.2 202.3 %reduce-scatter.24.cloned.1.call-start = ((), (), s32[]{:S(2)}) async-start(), calls=%async_computation.26 | async-start | bytes 1179648 | tf_op jit(solution)/shard_map/reduce_scatter | solution.py:268
  1050.4 288.8 %reduce-scatter.26.cloned.1.call-start = ((), (), s32[]{:S(2)}) async-start(), calls=%async_computation.27 | async-start | bytes 4718592 | tf_op jit(solution)/shard_map/reduce_scatter | solution.py:269
  1058.5 372.8 %reduce-scatter.20.cloned.1.call-start = ((), (), s32[]{:S(2)}) async-start(), calls=%async_computation.24 | async-start | bytes 4718592 | tf_op jit(solution)/shard_map/reduce_scatter | solution.py:266
  1065.1 650.3 %reduce-scatter.30.cloned.1.call-start = ((), (), s32[]{:S(2)}) async-start(), calls=%async_computation.29 | async-start | bytes 18874368 | tf_op jit(solution)/shard_map/reduce_scatter | solution.py:225
  1080.5 918.6 %reduce-scatter.28.cloned.1.call-start = ((), (), s32[]{:S(2)}) async-start(), calls=%async_computation.28 | async-start | bytes 18874368 | tf_op jit(solution)/shard_map/reduce_scatter | solution.py:224
  1096.1 1186.5 %reduce-scatter.32.cloned.1.call-start = ((), (), s32[]{:S(2)}) async-start(), calls=%async_computation.30 | async-start | bytes 18874368 | tf_op jit(solution)/shard_map/reduce_scatter | solution.py:226
  (35 other events, 336.7 us)
Sparse Core Ops, SparseCore 0:
  13.3 37.1 all-gather.9
  52.6 50.5 all-gather.11
  105.3 48.8 all-gather.13
  161.6 69.5 reduce-scatter.11
  233.2 124.4 all-gather.19
  359.7 32.6 all-gather.15
  394.5 124.4 all-gather.17
  521.1 32.6 all-gather.23
  555.8 124.9 all-gather.21
  729.6 69.5 reduce-scatter.15
  801.7 44.5 reduce-scatter.13
  851.1 34.4 all-gather.25
  1040.7 71.4 reduce-scatter.17
  1116.0 64.2 reduce-scatter.21
  1184.2 63.2 reduce-scatter.23
  1251.5 87.6 reduce-scatter.25
  1343.3 87.9 reduce-scatter.19
  1435.5 279.8 reduce-scatter.29
  1719.8 279.3 reduce-scatter.27
  2003.3 279.2 reduce-scatter.31
where the time goes:
time: 2300 us; the launch traced here: 2290 us
  waiting for transfers between devices  1770 us (77%)
  matrix products  271 us (12%)
  blocking collectives  105 us (5%)
  other arithmetic  64.5 us (3%)
  local copies, waits for them, and re-layouts  62 us (3%)
    reduce_scatter x1, waiting for transfers between devices, body(): lax.psum_scatter(grad_up, 'dp', scatter_dimension=0, tiled=True)  284 us
    reduce_scatter x1, waiting for transfers between devices, body(): lax.psum_scatter(grad_gate, 'dp', scatter_dimension=0, tiled=True)  284 us
    reduce_scatter x1, waiting for transfers between devices, body(): lax.psum_scatter(grad_down, 'dp', scatter_dimension=1, tiled=True)  284 us
    all_gather x1, waiting for transfers between devices, gather_mlp(): lax.all_gather(w_down, 'dp', axis=1, tiled=True)  127 us
    all_gather x1, waiting for transfers between devices, gather_mlp(): lax.all_gather(w_up, 'dp', axis=0, tiled=True)  119 us
    all_gather x1, waiting for transfers between devices, gather_mlp(): lax.all_gather(w_gate, 'dp', axis=0, tiled=True)  112 us
    reduce_scatter x1, waiting for transfers between devices, body(): lax.psum_scatter(grad_query, 'dp', scatter_dimension=0, tiled=True)  92 us
    reduce_scatter x1, waiting for transfers between devices, body(): lax.psum_scatter(grad_output, 'dp', scatter_dimension=1, tiled=True)  91.8 us
  transfers between devices with their start and end apart: 20, of which 19 were waited for; matrix products, arithmetic and copies ran while one was open for 8% of the time, Pallas kernels for 0%

commit v1 on v0

--- a/solution.py
+++ b/solution.py
@@ -7,6 +7,19 @@
 LEN = 1024
 epsilon = 1e-05
 theta = 500000.0
+
+
+def collect(shard, axis, dim):
+    count, here, span = (lax.axis_size(axis), lax.axis_index(axis), shard.shape[dim])
+    ahead = [(i, (i + 1) % count) for i in range(count)]
+    out = jnp.zeros((*shard.shape[:dim], count * span, *shard.shape[dim + 1 :]), shard.dtype)
+    block = shard
+    for turn in range(count):
+        owner = (here - turn) % count
+        out = lax.dynamic_update_slice_in_dim(out, block, owner * span, axis=dim)
+        if turn < count - 1:
+            block = lax.ppermute(block, axis, ahead)
+    return out
 
 
 def rope_frequencies():
@@ -52,7 +65,7 @@
 def gather_mlp(w_gate, w_up, w_down):
     return (
         lax.all_gather(w_gate, "dp", axis=0, tiled=True),
-        lax.all_gather(w_up, "dp", axis=0, tiled=True),
+        collect(w_up, "dp", 0),
         lax.all_gather(w_down, "dp", axis=1, tiled=True),
     )
 

time: 2300 us -> 2230 us (0.970)
  waiting for transfers between devices: 1770 us -> 1690 us
    ppermute x0 -> x7, waiting for transfers between devices: none -> 209 us  [collect(): block = lax.ppermute(block, axis, ahead)]
    all_gather x1 -> x0, waiting for transfers between devices: 119 us -> none  [gather_mlp(): lax.all_gather(w_up, 'dp', axis=0, tiled=True)]
    all_gather x1, waiting for transfers between devices: 127 us -> 42.1 us  [gather_mlp(): lax.all_gather(w_down, 'dp', axis=1, tiled=True)]
    reduce_scatter x1, waiting for transfers between devices: 69.1 us -> 0.01 us  [body(): lax.psum_scatter(jnp.dot(picked, output_all, preferred_element_type=jnp.f...]
  transfers between devices with their start and end apart: 20 -> 26, of which waited for: 19 -> 23; matrix products, arithmetic and copies ran while one was open for 8% -> 8% of each run, Pallas kernels for 0% -> 0%
where the time goes in v1:
time: 2230 us; the launch traced here: 2220 us
  waiting for transfers between devices  1690 us (76%)
  matrix products  264 us (12%)
  blocking collectives  105 us (5%)
  local copies, waits for them, and re-layouts  80.6 us (4%)
  other arithmetic  61.8 us (3%)
    reduce_scatter x1, waiting for transfers between devices, body(): lax.psum_scatter(grad_up, 'dp', scatter_dimension=0, tiled=True)  284 us
    reduce_scatter x1, waiting for transfers between devices, body(): lax.psum_scatter(grad_down, 'dp', scatter_dimension=1, tiled=True)  284 us
    reduce_scatter x1, waiting for transfers between devices, body(): lax.psum_scatter(grad_gate, 'dp', scatter_dimension=0, tiled=True)  284 us
    ppermute x7, waiting for transfers between devices, collect(): block = lax.ppermute(block, axis, ahead)  209 us
    all_gather x1, waiting for transfers between devices, gather_mlp(): lax.all_gather(w_gate, 'dp', axis=0, tiled=True)  112 us
    reduce_scatter x1, waiting for transfers between devices, body(): lax.psum_scatter(grad_query, 'dp', scatter_dimension=0, tiled=True)  92 us
    reduce_scatter x1, waiting for transfers between devices, body(): lax.psum_scatter(grad_output, 'dp', scatter_dimension=1, tiled=True)  91.7 us
    reduce_scatter x1, waiting for transfers between devices, body(): lax.psum_scatter(grad_value, 'dp', scatter_dimension=0, tiled=True)  67.1 us
  transfers between devices with their start and end apart: 26, of which 23 were waited for; matrix products, arithmetic and copies ran while one was open for 8% of the time, Pallas kernels for 0%

profile of v1, /device:TPU:0, one launch (start us, length us, event | category | flops | bytes accessed | tf_op | source)
XLA Modules:
  0.0 2222.2 jit_solution(7456830558008618177)
XLA Ops:
  15.9 33.1 %all_gather.38 = bf16[2048,128]{1,0:T(8,128)(2,1)S(1)} all-gather(bf16[256,128]{1,0:T(8,128)(2,1)S(1)} %copy-done.39), channel_id=1, replica_groups=mesh['dp'=8,'tensor'=4] {'dp'}, dimensions={0}, use_global_device_ids=true | all-gather | bytes 589824 | tf_op jit(solution)/shard_map/all_gather | solution.py:59
  48.9 31.7 %all_gather.39 = bf16[2048,128]{1,0:T(8,128)(2,1)S(1)} all-gather(bf16[256,128]{1,0:T(8,128)(2,1)S(1)} %copy-done.40), channel_id=1, replica_groups=mesh['dp'=8,'tensor'=4] {'dp'}, dimensions={0}, use_global_device_ids=true | all-gather | bytes 589824 | tf_op jit(solution)/shard_map/all_gather | solution.py:60
  112.8 30.8 %while.31 = (s32[]{:T(128)}, bf16[2,512,2,4,64]{1,4,3,2,0:T(8,128)(2,1)S(1)}, f32[2,2,4,512]{3,2,1,0:T(4,128)}, s32[2]{0:T(128)S(1)}, s32[1]{0:T(128)}, /*index=...) while((s32[]{:T(128)}, ...), condition=%wide.region_4.5_spmd, body=%wide.region_1.4_spmd.sunk | while | flops 1125119488 | bytes 54663480 | solution.py:108
  167.2 25.3 %collective-permute-done = bf16[256,2048]{1,0:T(8,128)(2,1)S(1)} collective-permute-done((bf16[256,2048]{1,0:T(8,128)(2,1)S(1)}, bf16[256,2048]{1,0:T(8,128)(2,1)S(1)}, u32[]{:S(2)}, u32[]{:S(2)}) %collective-permute-start) | collective-permute-done | bytes 1048608 | tf_op jit(solution)/shard_map/ppermute | solution.py:21
  192.5 25.9 %collective-permute-done.1 = bf16[256,2048]{1,0:T(8,128)(2,1)S(1)} collective-permute-done((bf16[256,2048]{1,0:T(8,128)(2,1)S(1)}, bf16[256,2048]{1,0:T(8,128)(2,1)S(1)}, u32[]{:S(2)}, u32[]{:S(2)}) %collective-permute-start.1) | collective-permute-done | bytes 1048608 | tf_op jit(solution)/shard_map/ppermute | solution.py:21
  219.3 25.1 %collective-permute-done.2 = bf16[256,2048]{1,0:T(8,128)(2,1)} collective-permute-done((bf16[256,2048]{1,0:T(8,128)(2,1)S(1)}, bf16[256,2048]{1,0:T(8,128)(2,1)}, u32[]{:S(2)}, u32[]{:S(2)}) %collective-permute-start.2) | collective-permute-done | bytes 1048608 | tf_op jit(solution)/shard_map/ppermute | solution.py:21
  247.7 21.2 collective-permute-done.3
  268.9 40.7 %collective-permute-done.4 = bf16[256,2048]{1,0:T(8,128)(2,1)S(1)} collective-permute-done((bf16[256,2048]{1,0:T(8,128)(2,1)}, bf16[256,2048]{1,0:T(8,128)(2,1)S(1)}, u32[]{:S(2)}, u32[]{:S(2)}) %collective-permute-start.4) | collective-permute-done | bytes 1048608 | tf_op jit(solution)/shard_map/ppermute | solution.py:21
  316.1 36.4 %collective-permute-done.5 = bf16[256,2048]{1,0:T(8,128)(2,1)} collective-permute-done((bf16[256,2048]{1,0:T(8,128)(2,1)S(1)}, bf16[256,2048]{1,0:T(8,128)(2,1)}, u32[]{:S(2)}, u32[]{:S(2)}) %collective-permute-start.5) | collective-permute-done | bytes 1048608 | tf_op jit(solution)/shard_map/ppermute | solution.py:21
  362.1 34.4 %collective-permute-done.6 = bf16[256,2048]{1,0:T(8,128)(2,1)S(1)} collective-permute-done((bf16[256,2048]{1,0:T(8,128)(2,1)}, bf16[256,2048]{1,0:T(8,128)(2,1)S(1)}, u32[]{:S(2)}, u32[]{:S(2)}) %collective-permute-start.6) | collective-permute-done | bytes 1048608 | tf_op jit(solution)/shard_map/ppermute | solution.py:21
  397.6 42.1 %all-gather.19.cloned.1.call-done = bf16[2048,2048]{1,0:T(8,128)(2,1)} async-done(((bf16[2048,256]{1,0:T(8,128)(2,1)}), bf16[2048,2048]{1,0:T(8,128)(2,1)}) %all-gather.19.cloned.1.call-update) | async-done | bytes 8388624 | tf_op jit(solution)/shard_map/all_gather | solution.py:69
  454.2 112.1 %all-gather.17.cloned.1.call-done = bf16[2048,2048]{1,0:T(8,128)(2,1)} async-done(((bf16[256,2048]{1,0:T(8,128)(2,1)}), bf16[2048,2048]{1,0:T(8,128)(2,1)}) %all-gather.17.cloned.1.call-update) | async-done | bytes 8388624 | tf_op jit(solution)/shard_map/all_gather | solution.py:67
  566.3 34.8 %all-gather.15.cloned.1.call-done = bf16[1024,2048]{1,0:T(8,128)(2,1)} async-done(((bf16[256,2048]{1,0:T(8,128)(2,1)}), bf16[1024,2048]{1,0:T(8,128)(2,1)}) %all-gather.15.cloned.1.call-update) | async-done | bytes 4194320 | tf_op jit(solution)/shard_map/all_gather | solution.py:205
  676.0 57.6 %reduce-scatter.16.cloned.1.call-done = f32[256,2048]{1,0:T(8,128)} async-done(((f32[1024,2048]{1,0:T(8,128)}), f32[256,2048]{1,0:T(8,128)}) %reduce-scatter.16.cloned.1.call-update) | async-done | bytes 2097168 | tf_op jit(solution)/shard_map/reduce_scatter | solution.py:241
  736.3 44.2 %reduce-scatter.14.cloned.1.call-done = bf16[256,2048]{1,0:T(8,128)(2,1)} async-done(((bf16[1024,2048]{1,0:T(8,128)(2,1)}), bf16[256,2048]{1,0:T(8,128)(2,1)}) %reduce-scatter.14.cloned.1.call-update) | async-done | bytes 1048592 | tf_op jit(solution)/shard_map/reduce_scatter | solution.py:212
  785.4 34.5 %all-gather.23.cloned.1.call-done = bf16[1024,2048]{1,0:T(8,128)(2,1)} async-done(((bf16[256,2048]{1,0:T(8,128)(2,1)}), bf16[1024,2048]{1,0:T(8,128)(2,1)}) %all-gather.23.cloned.1.call-update) | async-done | bytes 4194320 | tf_op jit(solution)/shard_map/all_gather | solution.py:256
  826.1 127.6 %while.32 = (s32[]{:T(128)}, f32[1024,2,64]{0,2,1:T(8,128)S(1)}, f32[1024,2,64]{0,2,1:T(8,128)}, f32[2,512,2,4,64]{1,0,4,3,2:T(2,128)}, s32[2]{0:T(128)S(1)}, /*...) while((s32[]{:T(128)}, f32[1024,2,64]{0,2,1:T(8,128)S(1)}, ...), condition=%wide.region_12.13_spmd.clone, body=%wide.region_10.12_spmd.clone.sunk | while | flops 2749232640 | bytes 181328368 | solution.py:147
  1047.3 40.1 %all-reduce.2 = (f32[2048]{0:T(1024)S(1)}, f32[2048]{0:T(1024)S(1)}) all-reduce(f32[2048]{0:T(1024)S(1)} %get-tuple-element.297, f32[2048]{0:T(1024)S(1)} %copy-done.41), channel_id=13, replica_groups=mesh['dp'=8,'tensor'=4] {'dp','tensor'}, use_global_device_ids=true, to_apply=%region_23.24.clone | all-reduce | flops 4096 | bytes 32768
  1113.0 67.1 %reduce-scatter.24.cloned.1.call-done = f32[256,128]{1,0:T(8,128)} async-done(((f32[2048,128]{1,0:T(8,128)}), f32[256,128]{1,0:T(8,128)}) %reduce-scatter.24.cloned.1.call-update) | async-done | bytes 131088 | tf_op jit(solution)/shard_map/reduce_scatter | solution.py:281
  1180.0 91.7 %reduce-scatter.26.cloned.1.call-done = f32[512,256]{1,0:T(8,128)} async-done(((f32[512,2048]{1,0:T(8,128)}), f32[512,256]{1,0:T(8,128)}) %reduce-scatter.26.cloned.1.call-update) | async-done | bytes 524304 | tf_op jit(solution)/shard_map/reduce_scatter | solution.py:282
  1271.8 92.0 %reduce-scatter.20.cloned.1.call-done = f32[256,512]{1,0:T(8,128)} async-done(((f32[2048,512]{1,0:T(8,128)}), f32[256,512]{1,0:T(8,128)}) %reduce-scatter.20.cloned.1.call-update) | async-done | bytes 524304 | tf_op jit(solution)/shard_map/reduce_scatter | solution.py:279
  1363.8 284.1 %reduce-scatter.30.cloned.1.call-done = f32[256,2048]{1,0:T(8,128)} async-done(((f32[2048,2048]{1,0:T(8,128)}), f32[256,2048]{1,0:T(8,128)}) %reduce-scatter.30.cloned.1.call-update) | async-done | bytes 2097168 | tf_op jit(solution)/shard_map/reduce_scatter | solution.py:238
  1647.9 283.5 %reduce-scatter.28.cloned.1.call-done = f32[256,2048]{1,0:T(8,128)} async-done(((f32[2048,2048]{1,0:T(8,128)}), f32[256,2048]{1,0:T(8,128)}) %reduce-scatter.28.cloned.1.call-update) | async-done | bytes 2097168 | tf_op jit(solution)/shard_map/reduce_scatter | solution.py:237
  1931.4 283.8 %reduce-scatter.32.cloned.1.call-done = f32[2048,256]{1,0:T(8,128)} async-done(((f32[2048,2048]{1,0:T(8,128)}), f32[2048,256]{1,0:T(8,128)}) %reduce-scatter.32.cloned.1.call-update) | async-done | bytes 2097168 | tf_op jit(solution)/shard_map/reduce_scatter | solution.py:239
  (277 shorter events, 461.3 us)
Async XLA Ops:
  7.2 73.4 %all-gather.9.cloned.1.call-start = ((), (), s32[]{:S(2)}) async-start(), calls=%async_computation.11 | async-start | bytes 5242880 | tf_op jit(solution)/shard_map/all_gather | solution.py:173
  13.2 90.3 %all-gather.11.cloned.1.call-start = ((), (), s32[]{:S(2)}) async-start(), calls=%async_computation.12 | async-start | bytes 2359296 | tf_op jit(solution)/shard_map/all_gather | solution.py:58
  13.9 140.6 %all-gather.13.cloned.1.call-start = ((), (), s32[]{:S(2)}) async-start(), calls=%async_computation.13 | async-start | bytes 2359296 | tf_op jit(solution)/shard_map/all_gather | solution.py:61
  14.7 229.8 %reduce-scatter.12.cloned.1.call-start = ((), (), s32[]{:S(2)}) async-start(), calls=%async_computation.14 | async-start | bytes 10485760 | tf_op jit(solution)/shard_map/reduce_scatter | solution.py:196
  161.9 235.7 %all-gather.21.cloned.1.call-start = ((), (), s32[]{:S(2)}) async-start(), calls=%async_computation.19 | async-start | bytes 5242880 | tf_op jit(solution)/shard_map/all_gather | solution.py:227
  164.3 275.4 %all-gather.19.cloned.1.call-start = ((), (), s32[]{:S(2)}) async-start(), calls=%async_computation.17 | async-start | bytes 9437184 | tf_op jit(solution)/shard_map/all_gather | solution.py:69
  164.8 401.4 %all-gather.17.cloned.1.call-start = ((), (), s32[]{:S(2)}) async-start(), calls=%async_computation.16 | async-start | bytes 9437184 | tf_op jit(solution)/shard_map/all_gather | solution.py:67
  165.6 435.5 %all-gather.15.cloned.1.call-start = ((), (), s32[]{:S(2)}) async-start(), calls=%async_computation.15 | async-start | bytes 5242880 | tf_op jit(solution)/shard_map/all_gather | solution.py:205
  165.6 26.8 %collective-permute-start = (bf16[256,2048]{1,0:T(8,128)(2,1)S(1)}, bf16[256,2048]{1,0:T(8,128)(2,1)S(1)}, u32[]{:S(2)}, u32[]{:S(2)}) collective-permute-start(bf16[256,2048]{1,0:T(8,128)(2,1)S(1)} %copy-done.25), channel_id=1, source_target_pairs={{0,4},{4,8},{8,12},{12,16},{16,20},{20,24},{24,28},{28,0},{1,5},{5... | collective-permute-start | bytes 3145736 | tf_op jit(solution)/shard_map/ppermute | solution.py:21
  192.4 25.9 %collective-permute-start.1 = (bf16[256,2048]{1,0:T(8,128)(2,1)S(1)}, bf16[256,2048]{1,0:T(8,128)(2,1)S(1)}, u32[]{:S(2)}, u32[]{:S(2)}) collective-permute-start(bf16[256,2048]{1,0:T(8,128)(2,1)S(1)} %collective-permute-done), channel_id=1, source_target_pairs={{0,4},{4,8},{8,12},{12,16},{16,20},{20,24},{24,28},{28,0},{1,5},{5... | collective-permute-start | bytes 3145736 | tf_op jit(solution)/shard_map/ppermute | solution.py:21
  247.7 486.0 %reduce-scatter.16.cloned.1.call-start = ((), (), s32[]{:S(2)}) async-start(), calls=%async_computation.20 | async-start | bytes 10485760 | tf_op jit(solution)/shard_map/reduce_scatter | solution.py:241
  268.9 40.7 %collective-permute-start.4 = (bf16[256,2048]{1,0:T(8,128)(2,1)}, bf16[256,2048]{1,0:T(8,128)(2,1)S(1)}, u32[]{:S(2)}, u32[]{:S(2)}) collective-permute-start(bf16[256,2048]{1,0:T(8,128)(2,1)} %collective-permute-done.3), channel_id=1, source_target_pairs={{0,4},{4,8},{8,12},{12,16},{16,20},{20,24},{24,28},{28,0},{1,5},{5... | collective-permute-start | bytes 3145736 | tf_op jit(solution)/shard_map/ppermute | solution.py:21
  309.6 42.9 %collective-permute-start.5 = (bf16[256,2048]{1,0:T(8,128)(2,1)S(1)}, bf16[256,2048]{1,0:T(8,128)(2,1)}, u32[]{:S(2)}, u32[]{:S(2)}) collective-permute-start(bf16[256,2048]{1,0:T(8,128)(2,1)S(1)} %collective-permute-done.4), channel_id=1, source_target_pairs={{0,4},{4,8},{8,12},{12,16},{16,20},{20,24},{24,28},{28,0},{1,5},{5... | collective-permute-start | bytes 3145736 | tf_op jit(solution)/shard_map/ppermute | solution.py:21
  352.5 44.0 %collective-permute-start.6 = (bf16[256,2048]{1,0:T(8,128)(2,1)}, bf16[256,2048]{1,0:T(8,128)(2,1)S(1)}, u32[]{:S(2)}, u32[]{:S(2)}) collective-permute-start(bf16[256,2048]{1,0:T(8,128)(2,1)} %collective-permute-done.5), channel_id=1, source_target_pairs={{0,4},{4,8},{8,12},{12,16},{16,20},{20,24},{24,28},{28,0},{1,5},{5... | collective-permute-start | bytes 3145736 | tf_op jit(solution)/shard_map/ppermute | solution.py:21
  662.1 118.5 %reduce-scatter.14.cloned.1.call-start = ((), (), s32[]{:S(2)}) async-start(), calls=%async_computation.18 | async-start | bytes 5242880 | tf_op jit(solution)/shard_map/reduce_scatter | solution.py:212
  676.0 143.9 %all-gather.23.cloned.1.call-start = ((), (), s32[]{:S(2)}) async-start(), calls=%async_computation.21 | async-start | bytes 5242880 | tf_op jit(solution)/shard_map/all_gather | solution.py:256
  785.3 259.3 %reduce-scatter.18.cloned.1.call-start = ((), (), s32[]{:S(2)}) async-start(), calls=%async_computation.22 | async-start | bytes 10485760 | tf_op jit(solution)/shard_map/reduce_scatter | solution.py:284
  973.1 139.9 %reduce-scatter.22.cloned.1.call-start = ((), (), s32[]{:S(2)}) async-start(), calls=%async_computation.24 | async-start | bytes 1179648 | tf_op jit(solution)/shard_map/reduce_scatter | solution.py:280
  977.6 202.4 %reduce-scatter.24.cloned.1.call-start = ((), (), s32[]{:S(2)}) async-start(), calls=%async_computation.25 | async-start | bytes 1179648 | tf_op jit(solution)/shard_map/reduce_scatter | solution.py:281
  982.8 288.9 %reduce-scatter.26.cloned.1.call-start = ((), (), s32[]{:S(2)}) async-start(), calls=%async_computation.26 | async-start | bytes 4718592 | tf_op jit(solution)/shard_map/reduce_scatter | solution.py:282
  991.0 372.8 %reduce-scatter.20.cloned.1.call-start = ((), (), s32[]{:S(2)}) async-start(), calls=%async_computation.23 | async-start | bytes 4718592 | tf_op jit(solution)/shard_map/reduce_scatter | solution.py:279
  997.6 650.3 %reduce-scatter.30.cloned.1.call-start = ((), (), s32[]{:S(2)}) async-start(), calls=%async_computation.28 | async-start | bytes 18874368 | tf_op jit(solution)/shard_map/reduce_scatter | solution.py:238
  1012.9 918.5 %reduce-scatter.28.cloned.1.call-start = ((), (), s32[]{:S(2)}) async-start(), calls=%async_computation.27 | async-start | bytes 18874368 | tf_op jit(solution)/shard_map/reduce_scatter | solution.py:237
  1028.5 1186.7 %reduce-scatter.32.cloned.1.call-start = ((), (), s32[]{:S(2)}) async-start(), calls=%async_computation.29 | async-start | bytes 18874368 | tf_op jit(solution)/shard_map/reduce_scatter | solution.py:239
  (56 other events, 1048.1 us)
Sparse Core Ops, SparseCore 0:
  13.3 37.1 all-gather.8
  52.6 50.8 all-gather.10
  105.6 48.8 all-gather.12
  161.9 69.5 reduce-scatter.11
  233.5 34.4 all-gather.20
  269.9 169.6 all-gather.18
  441.7 124.4 all-gather.16
  568.4 32.6 all-gather.14
  662.2 71.3 reduce-scatter.15
  736.0 44.5 reduce-scatter.13
  785.4 34.4 all-gather.22
  973.2 71.3 reduce-scatter.17
  1048.6 64.2 reduce-scatter.21
  1116.8 63.2 reduce-scatter.23
  1184.1 87.6 reduce-scatter.25
  1275.8 87.9 reduce-scatter.19
  1368.0 279.8 reduce-scatter.29
  1652.1 279.2 reduce-scatter.27
  1935.8 279.3 reduce-scatter.31
